TPU v7x, 256 devices: a whole 4x4x8 slice. The times are simulated.
256 devices in a mesh: sector: 16 (over z_lo, x, core), term: 16 (over z_hi, y).
Axes of the slice: x: 4, y: 4, z: 8 (z_hi: 4, z_lo: 2; z = z_hi * 2 + z_lo), core: 2. Of those that a mesh axis runs over, the one named last changes fastest.
Arguments:
- lanczos_vector: float32 [32, 512, 512], P('sector'), may hold values from -6 to 6
- left_block: bfloat16 [32, 64, 512, 512], P('sector', 'term'), may hold values from -0.375 to 0.375
- right_block: bfloat16 [32, 64, 512, 512], P('sector', 'term'), may hold values from -0.25 to 0.25
- left_energy: float32 [32, 512], P('sector'), may hold values from 0.5 to 4
- right_energy: float32 [32, 512], P('sector'), may hold values from 0.5 to 4
- sector_shifts: int32 [64], P('term'), may hold values from -1 to 1
- sector_sizes: int32 [32], P('sector'), may hold values from 128 to 512, as said below
Outputs:
- next_vector: float32 [32, 512, 512], P('sector', 'term')
- next_sigma: float32 [32, 512, 512], P('sector', 'term')
Inputs may be any that keep to these rules, and one draw needn't show every extreme that they name: `sector_sizes`: each value is a multiple of 128; some sector has exactly 512.
All inputs are finite; a program needn't handle non-finite values.
Results may differ from a plain program's by a relative error of at most 0.0023.
Values may be sent and summed in bfloat16 or wider, within the bound.
A program may use at most 64 MiB of HBM per device.

v0:
```python
import functools

import jax
import jax.numpy as jnp
from jax import lax
from jax.sharding import Mesh
from jax.sharding import PartitionSpec as P

TERM = ("term_0", "term_1")
SECTOR = ("sector_0", "sector_1", "sector_2")
SECTOR_TERM = ("sector_0", "sector_1", "sector_2", "term_0", "term_1")


epsilon = 1e-06


def padded(shard, sides, width):
    for axis, dim in sides:
        size, length = (lax.axis_size(axis), shard.shape[dim])
        up = [(i, (i + 1) % size) for i in range(size - 1)]
        down = [(j, i) for i, j in up]
        last = lax.slice_in_dim(shard, length - width, length, axis=dim)
        first = lax.slice_in_dim(shard, 0, width, axis=dim)
        before = lax.ppermute(last, axis, up)
        after = lax.ppermute(first, axis, down)
        shard = jnp.concatenate([before, shard, after], axis=dim)
    return shard


def split_up(shard, dim, length):
    before, after = (shard.shape[:dim], shard.shape[dim + 1 :])
    return jnp.moveaxis(shard.reshape(*before, length, -1, *after), dim, 0)


def sent_and_summed(shard, axis, dim):
    length = lax.axis_size(axis)
    tiles = lax.all_to_all(split_up(shard, dim, length), axis, 0, 0, tiled=True)
    return jnp.sum(tiles.astype(jnp.float32), axis=0)


def by_axis(shard, axes):
    return functools.reduce(lax.psum, axes, shard)


def copy_for_each(shard, axis):
    length = lax.axis_size(axis)
    return lax.all_to_all(
        jnp.broadcast_to(shard[None], (length, *shard.shape)), axis, 0, 0, tiled=True
    )


def in_order(tiles, dim):
    tiles = jnp.moveaxis(tiles, 0, dim)
    shape = tiles.shape
    return tiles.reshape(*shape[:dim], shape[dim] * shape[dim + 1], *shape[dim + 2 :])


def gather_directly(shard, axis, dim):
    tiles = copy_for_each(shard, axis)
    return in_order(tiles, dim)


def on_device(
    lanczos_vector, left_block, right_block, left_energy, right_energy, sector_shifts, sector_sizes
):
    sec_dev = lanczos_vector.shape[0]
    block_size = lanczos_vector.shape[1]
    term_dev = left_block.shape[1]
    term_count = lax.axis_size(TERM)
    term_scale = float(term_dev * term_count) ** (-0.5)
    cell_count = float(sec_dev * lax.axis_size(SECTOR) * block_size * block_size)
    row_span = block_size // term_count
    row_start = lax.axis_index(TERM) * row_span
    sector_positions = jnp.arange(block_size, dtype=jnp.int32)
    limits = sector_sizes[:, None, None]
    live_mask = (
        (sector_positions[None, :, None] < limits) & (sector_positions[None, None, :] < limits)
    ).astype(jnp.float32)
    energies = left_energy[:, :, None] + right_energy[:, None, :]
    neighbour = jnp.arange(sec_dev, dtype=jnp.int32)[None, :] + 1 + sector_shifts[:, None]

    def own_rows(blocks):
        return lax.dynamic_slice_in_dim(blocks, row_start, row_span, 1)

    mask_local, energy_local = (own_rows(live_mask), own_rows(energies))

    def partial_terms(full_blocks):
        extended = padded(full_blocks.astype(jnp.bfloat16), ((SECTOR, 0),), 1)
        paired_sectors = jnp.take(extended, neighbour, axis=0)
        left_blended = jnp.einsum(
            "stab,tsbc->stac", left_block, paired_sectors, preferred_element_type=jnp.float32
        ).astype(jnp.bfloat16)
        return jnp.einsum(
            "stac,stdc->sad", left_blended, right_block, preferred_element_type=jnp.float32
        )

    def apply_hamiltonian(full_blocks):
        partials = partial_terms(full_blocks)
        summed = sent_and_summed(partials.astype(jnp.bfloat16), TERM, 1)
        local_blocks = own_rows(full_blocks)
        return (local_blocks, mask_local * (energy_local * local_blocks + term_scale * summed))

    def reduce_stats(values):
        return jax.tree.map(lambda part: by_axis(part, SECTOR_TERM), values)

    start_vector = live_mask * lanczos_vector
    start_local, sigma = apply_hamiltonian(start_vector)
    correlation, norm_sq = reduce_stats(
        (jnp.sum(start_local * sigma), jnp.sum(start_local * start_local))
    )
    ritz_value = correlation / cell_count / (norm_sq / cell_count + epsilon)
    residual = sigma - ritz_value * start_local
    res_parts = reduce_stats((jnp.sum(residual * residual),))
    res_sq = res_parts[0]
    next_local = residual / jnp.sqrt(res_sq / cell_count + epsilon)
    next_full = gather_directly(next_local, TERM, 1)
    unused_rows, next_sigma = apply_hamiltonian(next_full)
    return (next_local, next_sigma)


def solution(mesh):
    finer = Mesh(
        mesh.devices.reshape(2, 4, 2, 4, 4),
        ("sector_0", "sector_1", "sector_2", "term_0", "term_1"),
    )
    return jax.shard_map(
        on_device,
        mesh=finer,
        in_specs=(
            P(SECTOR, None, None),
            P(SECTOR, TERM, None, None),
            P(SECTOR, TERM, None, None),
            P(SECTOR, None),
            P(SECTOR, None),
            P(TERM),
            P(SECTOR),
        ),
        out_specs=(P(SECTOR, TERM, None), P(SECTOR, TERM, None)),
        check_vma=False,
    )
```

profile of v0, /device:TPU:3, one launch (start us, length us, event | category | flops | bytes accessed | tf_op | source)
XLA Modules:
  0.0 283.3 jit_solution(6663998264110081141)
XLA Ops:
  0.7 0.7 iota_compare_fusion
  1.4 3.3 %fusion.38 = (bf16[2,512,512]{2,1,0:T(8,128)(2,1)S(1)}, f32[2,512,512]{2,1,0:T(8,128)}) fusion(f32[2,512,512]{2,1,0:T(8,128)} %param.9, pred[2,512]{1,0:T(4,128)(4,1)S(1)} %iota_compare_fusion), kind=kLoop, calls=%fused_computation.46 | loop fusion | flops 1572864 | bytes 5243904 | tf_op jit(solution)/shard_map/convert_element_type | solution.py:88
  4.8 3.7 %collective-permute-start = (bf16[1,512,512]{2,1,0:T(8,128)(2,1)S(1)}, bf16[1,512,512]{2,1,0:T(8,128)(2,1)S(1)}, u32[]{:S(2)}, u32[]{:S(2)}) collective-permute-start(bf16[1,512,512]{2,1,0:T(8,128)(2,1)S(1)} %get-tuple-element.19), channel_id=1, source_target_pairs={{0,16},{16,32},{32,48},{48,64},{64,80},{80,96},{96,112},{112,128},... | collective-permute-start | bytes 1572872 | tf_op jit(solution)/shard_map/ppermute | solution.py:24
  8.4 1.9 collective-permute-start.1
  10.4 0.1 compare_and_fusion
  10.5 0.1 copy.17
  10.7 0.1 reshape.95
  10.8 3.8 %collective-permute-done = bf16[1,512,512]{2,1,0:T(8,128)(2,1)S(1)} collective-permute-done((bf16[1,512,512]{2,1,0:T(8,128)(2,1)S(1)}, bf16[1,512,512]{2,1,0:T(8,128)(2,1)S(1)}, u32[]{:S(2)}, u32[]{:S(2)}) %collective-permute-start) | collective-permute-done | bytes 524320 | tf_op jit(solution)/shard_map/ppermute | solution.py:24
  14.6 0.8 copy-done.3
  15.4 3.7 %collective-permute-done.1 = bf16[1,512,512]{2,1,0:T(8,128)(2,1)} collective-permute-done((bf16[1,512,512]{2,1,0:T(8,128)(2,1)S(1)}, bf16[1,512,512]{2,1,0:T(8,128)(2,1)}, u32[]{:S(2)}, u32[]{:S(2)}) %collective-permute-start.1) | collective-permute-done | bytes 524320 | tf_op jit(solution)/shard_map/ppermute | solution.py:25
  19.1 1.4 pad_maximum_fusion
  20.5 2.7 gather_fusion
  23.2 7.3 %copy.18 = bf16[4,2,512,512]{2,3,0,1:T(8,128)(2,1)} copy(bf16[4,2,512,512]{3,2,1,0:T(8,128)(2,1)} %bitcast.35) | data formatting | bytes 8388608 | tf_op jit(solution)/shard_map/jit(_take)/gather | solution.py:89
  30.5 9.2 %bitcast_convert_fusion.1 = bf16[2,512,512]{2,1,0:T(8,128)(2,1)S(1)} fusion(bf16[2,4,512,512]{3,2,1,0:T(8,128)(2,1)} %param.11, bf16[2,4,512,512]{3,2,1,0:T(8,128)(2,1)} %param.10, bf16[4,2,512,512]{2,3,0,1:T(8,128)(2,1)} %copy.18, pred[4,2]{0,1:T(4,128)(4,1)S(1)} %copy.17), kind=kOutput, calls=%fused_computation.17 | convolution fusion | flops 4299685888 | bytes 13631496 | tf_op jit(solution)/shard_map/stac,stdc->sad/dot_general | solution.py:93
  39.8 1.1 copy.33
  40.8 10.9 %all-to-all-start = ((bf16[16,2,32,512]{3,2,1,0:T(8,128)(2,1)}), bf16[16,2,32,512]{3,2,1,0:T(8,128)(2,1)S(1)}, u32[]{:S(2)}, u32[]{:S(2)}) async-start(bf16[16,2,32,512]{3,2,1,0:T(8,128)(2,1)} %bitcast.33), calls=%async_computation | async-start | bytes 2097152 | tf_op jit(solution)/shard_map/all_to_all | solution.py:37
  51.8 0.3 broadcast_and_fusion
  52.2 26.7 %all-to-all-done = bf16[16,2,32,512]{3,2,1,0:T(8,128)(2,1)S(1)} async-done(((bf16[16,2,32,512]{3,2,1,0:T(8,128)(2,1)}), bf16[16,2,32,512]{3,2,1,0:T(8,128)(2,1)S(1)}, u32[]{:S(2)}, u32[]{:S(2)}) %all-to-all-start) | async-done | bytes 1048608 | tf_op jit(solution)/shard_map/all_to_all | solution.py:37
  78.9 0.1 convert_reduce_fusion.1
  79.1 1.6 multiply_reduce_fusion.1
  80.7 5.4 %all-reduce.4 = (f32[]{:T(128)}, f32[]{:T(128)}) all-reduce(f32[]{:T(128)} %get-tuple-element.4, f32[]{:T(128)} %get-tuple-element.3), channel_id=1, replica_groups=mesh['sector_0'=2,'sector_1'=4,'sector_2'=2,'term_0'=4,'term_1'=4] {'sec..., use_global_device_ids=true, to_apply=%region_2.4 | all-reduce | flops 2 | bytes 16 | tf_op jit(solution)/shard_map/psum | solution.py:42
  86.1 7.2 %all-reduce.2 = (f32[]{:T(128)}, f32[]{:T(128)}) all-reduce(f32[]{:T(128)} %get-tuple-element.13, f32[]{:T(128)} %get-tuple-element.14), channel_id=1, replica_groups=mesh['sector_0'=2,'sector_1'=4,'sector_2'=2,'term_0'=4,'term_1'=4] {'sec..., use_global_device_ids=true, to_apply=%region_3.5 | all-reduce | flops 2 | bytes 16 | tf_op jit(solution)/shard_map/psum | solution.py:42
  93.3 6.0 %all-reduce.3 = (f32[]{:T(128)}, f32[]{:T(128)}) all-reduce(f32[]{:T(128)} %get-tuple-element.9, f32[]{:T(128)} %get-tuple-element.10), channel_id=1, replica_groups=mesh['sector_0'=2,'sector_1'=4,'sector_2'=2,'term_0'=4,'term_1'=4] {'sec..., use_global_device_ids=true, to_apply=%region_4.6 | all-reduce | flops 2 | bytes 16 | tf_op jit(solution)/shard_map/psum | solution.py:42
  99.3 9.9 %all-reduce.1 = (f32[]{:T(128)}, f32[]{:T(128)}) all-reduce(f32[]{:T(128)} %get-tuple-element.11, f32[]{:T(128)} %get-tuple-element.12), channel_id=1, replica_groups=mesh['sector_0'=2,'sector_1'=4,'sector_2'=2,'term_0'=4,'term_1'=4] {'ter..., use_global_device_ids=true, to_apply=%region_5.7 | all-reduce | flops 2 | bytes 16 | tf_op jit(solution)/shard_map/psum | solution.py:42
  109.2 7.8 %all-reduce = (f32[]{:T(128)}, f32[]{:T(128)}) all-reduce(f32[]{:T(128)} %get-tuple-element.7, f32[]{:T(128)} %get-tuple-element.8), channel_id=1, replica_groups=mesh['sector_0'=2,'sector_1'=4,'sector_2'=2,'term_0'=4,'term_1'=4] {'ter..., use_global_device_ids=true, to_apply=%region_6.8 | all-reduce | flops 2 | bytes 16 | tf_op jit(solution)/shard_map/psum | solution.py:42
  118.3 1.6 multiply_reduce_fusion
  120.0 4.4 %psum.115 = f32[]{:T(128)} all-reduce(f32[]{:T(128)} %multiply_reduce_fusion), channel_id=1, replica_groups=mesh['sector_0'=2,'sector_1'=4,'sector_2'=2,'term_0'=4,'term_1'=4] {'sec..., use_global_device_ids=true, to_apply=%region_14.16 | all-reduce | flops 1 | bytes 8 | tf_op jit(solution)/shard_map/psum | solution.py:42
  124.4 6.9 %psum.116 = f32[]{:T(128)} all-reduce(f32[]{:T(128)} %psum.115), channel_id=1, replica_groups=mesh['sector_0'=2,'sector_1'=4,'sector_2'=2,'term_0'=4,'term_1'=4] {'sec..., use_global_device_ids=true, to_apply=%region_15.17 | all-reduce | flops 1 | bytes 8 | tf_op jit(solution)/shard_map/psum | solution.py:42
  131.3 10.3 %psum.117 = f32[]{:T(128)} all-reduce(f32[]{:T(128)} %psum.116), channel_id=1, replica_groups=mesh['sector_0'=2,'sector_1'=4,'sector_2'=2,'term_0'=4,'term_1'=4] {'sec..., use_global_device_ids=true, to_apply=%region_16.18 | all-reduce | flops 1 | bytes 8 | tf_op jit(solution)/shard_map/psum | solution.py:42
  141.5 8.1 %psum.118 = f32[]{:T(128)} all-reduce(f32[]{:T(128)} %psum.117), channel_id=1, replica_groups=mesh['sector_0'=2,'sector_1'=4,'sector_2'=2,'term_0'=4,'term_1'=4] {'ter..., use_global_device_ids=true, to_apply=%region_17.19 | all-reduce | flops 1 | bytes 8 | tf_op jit(solution)/shard_map/psum | solution.py:42
  149.6 6.8 %psum.119 = f32[]{:T(128)} all-reduce(f32[]{:T(128)} %psum.118), channel_id=1, replica_groups=mesh['sector_0'=2,'sector_1'=4,'sector_2'=2,'term_0'=4,'term_1'=4] {'ter..., use_global_device_ids=true, to_apply=%region_18.20 | all-reduce | flops 1 | bytes 8 | tf_op jit(solution)/shard_map/psum | solution.py:42
  157.1 1.0 broadcast_divide_fusion
  158.2 0.3 broadcast_in_dim.8
  158.4 45.7 %all_to_all.15 = f32[16,2,32,512]{3,2,1,0:T(8,128)S(1)} all-to-all(f32[16,2,32,512]{3,2,1,0:T(8,128)S(1)} %broadcast_in_dim.8), channel_id=1, replica_groups=mesh['sector_0'=2,'sector_1'=4,'sector_2'=2,'term_0'=4,'term_1'=4] {'ter..., dimensions={0} | all-to-all | bytes 4194304 | tf_op jit(solution)/shard_map/all_to_all | solution.py:47
  204.1 0.3 copy.21
  204.4 0.1 bitcast_convert_fusion.2
  204.6 14.0 %collective-permute-start.2 = (bf16[1,512,512]{2,1,0:T(8,128)(2,1)S(1)}, bf16[1,512,512]{2,1,0:T(8,128)(2,1)S(1)}, u32[]{:S(2)}, u32[]{:S(2)}) collective-permute-start(bf16[1,512,512]{2,1,0:T(8,128)(2,1)S(1)} %get-tuple-element.17), channel_id=1, source_target_pairs={{0,16},{16,32},{32,48},{48,64},{64,80},{80,96},{96,112},{112,128},... | collective-permute-start | bytes 1572872 | tf_op jit(solution)/shard_map/ppermute | solution.py:24
  218.6 2.1 collective-permute-start.3
  220.7 4.0 %collective-permute-done.2 = bf16[1,512,512]{2,1,0:T(8,128)(2,1)S(1)} collective-permute-done((bf16[1,512,512]{2,1,0:T(8,128)(2,1)S(1)}, bf16[1,512,512]{2,1,0:T(8,128)(2,1)S(1)}, u32[]{:S(2)}, u32[]{:S(2)}) %collective-permute-start.2) | collective-permute-done | bytes 524320 | tf_op jit(solution)/shard_map/ppermute | solution.py:24
  224.7 4.4 %collective-permute-done.3 = bf16[1,512,512]{2,1,0:T(8,128)(2,1)S(1)} collective-permute-done((bf16[1,512,512]{2,1,0:T(8,128)(2,1)S(1)}, bf16[1,512,512]{2,1,0:T(8,128)(2,1)S(1)}, u32[]{:S(2)}, u32[]{:S(2)}) %collective-permute-start.3) | collective-permute-done | bytes 524320 | tf_op jit(solution)/shard_map/ppermute | solution.py:25
  229.1 0.2 pad_maximum_fusion.1
  229.4 2.7 gather_fusion.1
  232.1 7.3 %copy.23 = bf16[4,2,512,512]{2,3,0,1:T(8,128)(2,1)} copy(bf16[4,2,512,512]{3,2,1,0:T(8,128)(2,1)} %bitcast.34) | data formatting | bytes 8388608 | tf_op jit(solution)/shard_map/jit(_take)/gather | solution.py:89
  239.4 9.2 %bitcast_convert_fusion = bf16[2,512,512]{2,1,0:T(8,128)(2,1)S(1)} fusion(bf16[2,4,512,512]{3,2,1,0:T(8,128)(2,1)} %param.11, bf16[2,4,512,512]{3,2,1,0:T(8,128)(2,1)} %param.10, bf16[4,2,512,512]{2,3,0,1:T(8,128)(2,1)} %copy.23, pred[4,2]{0,1:T(4,128)(4,1)S(1)} %copy.17), kind=kOutput, calls=%fused_computation.16 | convolution fusion | flops 4299685888 | bytes 13631496 | tf_op jit(solution)/shard_map/stac,stdc->sad/dot_general | solution.py:93
  248.6 0.1 copy.32
  248.7 32.8 %all_to_all.16 = bf16[16,2,32,512]{3,2,1,0:T(8,128)(2,1)S(1)} all-to-all(bf16[16,2,32,512]{3,2,1,0:T(8,128)(2,1)S(1)} %bitcast.37), channel_id=1, replica_groups=mesh['sector_0'=2,'sector_1'=4,'sector_2'=2,'term_0'=4,'term_1'=4] {'ter..., dimensions={0} | all-to-all | bytes 2097152 | tf_op jit(solution)/shard_map/all_to_all | solution.py:37
  281.5 0.1 convert_reduce_fusion
  281.6 1.7 convert_multiply_fusion.1
  (17 shorter events, 0.3 us)
Async XLA Ops:
  0.6 51.1 %copy-start = (f32[2,512]{1,0:T(2,128)S(1)}, f32[2,512]{1,0:T(2,128)}, u32[]{:S(2)}) copy-start(f32[2,512]{1,0:T(2,128)} %param.12) | copy-start | bytes 12292
  0.6 9.7 %copy-start.5 = (s32[4]{0:T(128)S(1)}, s32[4]{0:T(128)}, u32[]{:S(2)}) copy-start(s32[4]{0:T(128)} %param.14) | copy-start | bytes 52
  4.8 9.8 %collective-permute-start = (bf16[1,512,512]{2,1,0:T(8,128)(2,1)S(1)}, bf16[1,512,512]{2,1,0:T(8,128)(2,1)S(1)}, u32[]{:S(2)}, u32[]{:S(2)}) collective-permute-start(bf16[1,512,512]{2,1,0:T(8,128)(2,1)S(1)} %get-tuple-element.19), channel_id=1, source_target_pairs={{0,16},{16,32},{32,48},{48,64},{64,80},{80,96},{96,112},{112,128},... | collective-permute-start | bytes 1572872 | tf_op jit(solution)/shard_map/ppermute | solution.py:24
  8.4 10.6 %collective-permute-start.1 = (bf16[1,512,512]{2,1,0:T(8,128)(2,1)S(1)}, bf16[1,512,512]{2,1,0:T(8,128)(2,1)}, u32[]{:S(2)}, u32[]{:S(2)}) collective-permute-start(bf16[1,512,512]{2,1,0:T(8,128)(2,1)S(1)} %get-tuple-element.20), channel_id=1, source_target_pairs={{16,0},{32,16},{48,32},{64,48},{80,64},{96,80},{112,96},{128,112},... | collective-permute-start | bytes 1572872 | tf_op jit(solution)/shard_map/ppermute | solution.py:25
  14.6 0.8 copy-start.3
  39.7 39.3 %copy-start.4 = (f32[2,512]{1,0:T(2,128)S(1)}, f32[2,512]{1,0:T(2,128)}, u32[]{:S(2)}) copy-start(f32[2,512]{1,0:T(2,128)} %param.13) | copy-start | bytes 12292
  40.8 38.1 %all-to-all-start = ((bf16[16,2,32,512]{3,2,1,0:T(8,128)(2,1)}), bf16[16,2,32,512]{3,2,1,0:T(8,128)(2,1)S(1)}, u32[]{:S(2)}, u32[]{:S(2)}) async-start(bf16[16,2,32,512]{3,2,1,0:T(8,128)(2,1)} %bitcast.33), calls=%async_computation | async-start | bytes 2097152 | tf_op jit(solution)/shard_map/all_to_all | solution.py:37
  158.1 46.2 %copy-start.2 = (f32[2,32,512]{2,1,0:T(8,128)}, f32[2,32,512]{2,1,0:T(8,128)S(1)}, u32[]{:S(2)}) copy-start(f32[2,32,512]{2,1,0:T(8,128)S(1)} %broadcast_divide_fusion) | copy-start | bytes 393220
  204.4 20.3 %copy-start.1 = (f32[16,2,32,512]{3,2,0,1:T(8,128)}, f32[16,2,32,512]{3,2,0,1:T(8,128)S(1)}, u32[]{:S(2)}) copy-start(f32[16,2,32,512]{3,2,0,1:T(8,128)S(1)} %copy.21) | copy-start | bytes 6291460
  204.6 20.1 %collective-permute-start.2 = (bf16[1,512,512]{2,1,0:T(8,128)(2,1)S(1)}, bf16[1,512,512]{2,1,0:T(8,128)(2,1)S(1)}, u32[]{:S(2)}, u32[]{:S(2)}) collective-permute-start(bf16[1,512,512]{2,1,0:T(8,128)(2,1)S(1)} %get-tuple-element.17), channel_id=1, source_target_pairs={{0,16},{16,32},{32,48},{48,64},{64,80},{80,96},{96,112},{112,128},... | collective-permute-start | bytes 1572872 | tf_op jit(solution)/shard_map/ppermute | solution.py:24
  218.6 10.5 %collective-permute-start.3 = (bf16[1,512,512]{2,1,0:T(8,128)(2,1)S(1)}, bf16[1,512,512]{2,1,0:T(8,128)(2,1)S(1)}, u32[]{:S(2)}, u32[]{:S(2)}) collective-permute-start(bf16[1,512,512]{2,1,0:T(8,128)(2,1)S(1)} %get-tuple-element.18), channel_id=1, source_target_pairs={{16,0},{32,16},{48,32},{64,48},{80,64},{96,80},{112,96},{128,112},... | collective-permute-start | bytes 1572872 | tf_op jit(solution)/shard_map/ppermute | solution.py:25
where the time goes:
time: 284 us; the launch traced here: 283 us
  blocking collectives  151 us (53%)
  waiting for transfers between devices  42.6 us (15%)
  starting transfers between devices  32.6 us (11%)
  local copies, waits for them, and re-layouts  23 us (8%)
  matrix products  18.4 us (6%)
  other arithmetic  12.5 us (4%)
  between operations  2.89 us (1%)
    psum x10, blocking collectives, by_axis(): return functools.reduce(lax.psum, axes, shard)  72.8 us
    all_to_all x1, blocking collectives, copy_for_each(): lax.all_to_all(jnp.broadcast_to(shard[None], (length, *shard.shape)), axi...  45.7 us
    all_to_all x1, blocking collectives, sent_and_summed(): tiles = lax.all_to_all(split_up(shard, dim, length), axis, 0, 0, tiled=True)  32.8 us
    all_to_all x1, waiting for transfers between devices, sent_and_summed(): tiles = lax.all_to_all(split_up(shard, dim, length), axis, 0, 0, tiled=True)  26.7 us
    gather x4, local copies, waits for them, and re-layouts, partial_terms(): paired_sectors = jnp.take(extended, neighbour, axis=0)  20.1 us
    dot_general x2, matrix products, partial_terms(): jnp.einsum('stac,stdc->sad', left_blended, right_block, preferred_element...  18.4 us
    ppermute x2, starting transfers between devices, padded(): before = lax.ppermute(last, axis, up)  17.7 us
    all_to_all x1, starting transfers between devices, sent_and_summed(): tiles = lax.all_to_all(split_up(shard, dim, length), axis, 0, 0, tiled=True)  10.9 us
  transfers between devices with their start and end apart: 5, of which 5 were waited for; matrix products, arithmetic and copies ran while one was open for 0% of the time, Pallas kernels for 0%

commit v1 on v0

v1 whole, which is shorter than its diff:
```python
import functools

import jax
import jax.numpy as jnp
from jax import lax
from jax.experimental import pallas as pl
from jax.experimental.pallas import tpu as pltpu
from jax.sharding import Mesh
from jax.sharding import PartitionSpec as P

TERM = ("term_0", "term_1")
SECTOR = ("sector_0", "sector_1", "sector_2")
MESH = pl.DeviceIdType.MESH
F32, BF16 = jnp.float32, jnp.bfloat16
EPSILON = 1e-06
COPIES = 240


def fold(values):
    total = None
    for j in range(values.shape[0]):
        for r in range(0, values.shape[1], 8):
            for c in range(0, values.shape[2], 128):
                piece = values[j, r : r + 8, c : c + 128]
                total = piece if total is None else total + piece
    return total


def kernel(
    dims,
    shifts,
    sizes,
    left_energy,
    right_energy,
    v_hbm,
    left_hbm,
    right_hbm,
    next_out,
    sigma_out,
    v_full,
    v_rows,
    left,
    right,
    wide_v,
    wide_u,
    opp_tx,
    relay_rx,
    dir_tx,
    dir_rx,
    sum_tx,
    sum_rx,
    near,
    own,
    z_tx,
    z_rx,
    rows_f32,
    stat_tx,
    stat_rx,
    load_sem,
    send_sem,
    recv_sem,
):
    n_lo, n_x, n_core, n_z, n_y = dims
    terms = left.shape[1]
    span, width = v_rows.shape[1], v_rows.shape[2]
    n_sec = n_lo * n_x * n_core
    block = n_z * n_y * span
    scale = float(terms * n_z * n_y) ** (-0.5)
    cells = float(2 * n_sec * block * width)

    lo, x, core = [lax.axis_index(a) for a in SECTOR]
    z, y = [lax.axis_index(a) for a in TERM]
    sec = (lo * n_x + x) * n_core + core
    rank = z * n_y + y
    zs = [lax.rem(z + k, n_z) for k in range(n_z)]
    ys = [lax.rem(y + k, n_y) for k in range(n_y)]
    zp, zo, zm = zs[1], zs[2], zs[3]
    yp, yo, ym = ys[1], ys[2], ys[3]
    y_to = [{"term_1": yp}, {"term_1": ym}]
    z_to = [{"term_0": zp}, {"term_0": zm}]

    def sector_device(s):
        s = lax.rem(s, n_sec)
        return {
            "sector_0": s // (n_x * n_core),
            "sector_1": lax.rem(s // n_core, n_x),
            "sector_2": lax.rem(s, n_core),
        }

    below, above = sector_device(sec + n_sec - 1), sector_device(sec + 1)
    axes = [
        ("sector_2", n_core, core),
        ("sector_1", n_x, x),
        ("term_1", n_y, y),
        ("sector_0", n_lo, lo),
        ("term_0", n_z, z),
    ]

    loads = [pltpu.make_async_copy(v_hbm.at[:, rank], v_rows, load_sem.at[0])]
    for j in range(2):
        loads.append(pltpu.make_async_copy(v_hbm.at[j], v_full.at[j], load_sem.at[1 + j]))
    loads.append(pltpu.make_async_copy(left_hbm, left, load_sem.at[3]))
    loads.append(pltpu.make_async_copy(right_hbm, right, load_sem.at[4]))
    for load in loads:
        load.start()

    barrier = pltpu.get_barrier_semaphore()
    peers = [below, above]
    for name, size, me in axes:
        peers += [{name: lax.rem(me + k, size)} for k in range(1, size)]
    for peer in peers:
        pl.semaphore_signal(barrier, inc=1, device_id=peer, device_id_type=MESH)

    copies = {}

    def send(key, src, dst, to):
        index = len(copies)
        copies[key] = pltpu.make_async_remote_copy(
            src_ref=src,
            dst_ref=dst,
            send_sem=send_sem.at[index],
            recv_sem=recv_sem.at[index],
            device_id=to,
            device_id_type=MESH,
        )
        copies[key].start()

    def arrived(*keys):
        for key in keys:
            copies[key].wait_recv()

    def stat_send(run, stage):
        name, size, me = axes[stage]
        for k in range(1, size):
            send(
                ("stat", run, stage, k),
                stat_tx.at[run, stage],
                stat_rx.at[run, stage, k - 1],
                {name: lax.rem(me + k, size)},
            )

    def stat_sum(run, stage):
        size = axes[stage][1]
        total = stat_tx[run, stage]
        for k in range(1, size):
            arrived(("stat", run, stage, k))
            total = total + stat_rx[run, stage, k - 1]
        stat_tx[run, stage + 1] = total
        if stage + 1 < len(axes):
            stat_send(run, stage + 1)

    def total_of(run, which):
        return jnp.sum(stat_tx[run, len(axes), which], keepdims=True)

    row = lax.broadcasted_iota(jnp.int32, (span, width), 0) + rank * span
    col = lax.broadcasted_iota(jnp.int32, (span, width), 1)
    masks, energies = [], []
    for j in range(2):
        masks.append((row < sizes[j]) & (col < sizes[j]))
        le = jnp.where(row == col, left_energy[j : j + 1, :], 0.0)
        energies.append(jnp.sum(le, axis=1, keepdims=True) + right_energy[j : j + 1, :])

    zero = jnp.zeros((n_y, span, width), BF16)
    for k in range(n_z):
        wide_v[4, k] = zero
        wide_u[4, k] = zero
    pl.semaphore_wait(barrier, len(peers))
    for j in range(2):
        loads[1 + j].wait()
        for k in range(n_z * n_y):
            r = lax.broadcasted_iota(jnp.int32, (span, width), 0) + k * span
            keep = (r < sizes[j]) & (col < sizes[j])
            wide_v[1 + j, k // n_y, k % n_y] = jnp.where(keep, v_full[j, k], 0.0).astype(BF16)
        send(("halo", j), wide_v.at[1 + j], wide_v.at[3 if j == 0 else 0], below if j == 0 else above)

    loads[0].wait()
    squares, weighted = [], []
    for j in range(2):
        v = jnp.where(masks[j], v_rows[j], 0.0)
        v_rows[j] = v
        squares.append(v * v)
        weighted.append(v * v * energies[j])
    stat_tx[0, 0, 0] = fold(jnp.stack(squares))
    stat_tx[0, 0, 1] = fold(jnp.stack(weighted))
    stat_send(0, 0)

    slots = []
    for j in range(2):
        for t in range(terms):
            p = 1 + j + shifts[t]
            outside = ((sec == 0) & (p == 0)) | ((sec == n_sec - 1) & (p == 3))
            slots.append(jnp.where(outside, 4, p))

    def chunk(vector, j, yy):
        total = jnp.zeros((n_z * span, block), F32)
        for t in range(terms):
            rows = left[j, t, :, yy].reshape(n_z * span, block)
            paired = vector[slots[j * terms + t]].reshape(block, width)
            mixed = jnp.dot(rows, paired, preferred_element_type=F32).astype(BF16)
            total = total + lax.dot_general(
                mixed, right[j, t], (((1,), (1,)), ((), ())), preferred_element_type=F32
            )
        return total.reshape(n_z, span, block)

    def summed_terms(run, vector, between):
        order = [zo, zp, zm, z]
        for j in range(2):
            opp_tx[run, j] = chunk(vector, j, yo).astype(BF16)
        for k, zz in enumerate(order):
            for d in range(2):
                send(("relay", run, k, d), opp_tx.at[run, d, zz], relay_rx.at[run, d, zz], y_to[d])

        def direct(k):
            for d in range(2):
                send(("dir", run, k, d), dir_tx.at[run, d, order[k]], dir_rx.at[run, d, order[k]], y_to[d])

        between(0)
        dir_tx[run, 0] = chunk(vector, 1, yp).astype(BF16)
        dir_tx[run, 1] = chunk(vector, 0, ym).astype(BF16)
        direct(0)
        between(1)
        near[0] = chunk(vector, 0, yp)
        near[1] = chunk(vector, 1, ym)
        for k, zz in enumerate(order):
            if k:
                direct(k)
            for d in range(2):
                arrived(("relay", run, k, d))
                sum_tx[run, d, zz] = (near[d, zz] + relay_rx[run, d, zz].astype(F32)).astype(BF16)
                send(("sum", run, k, d), sum_tx.at[run, d, zz], sum_rx.at[run, d, zz], y_to[d])
        between(2)
        for j in range(2):
            own[j] = chunk(vector, j, y)
        between(3)

        def collect(k):
            zz = order[k]
            arrived(*[(kind, run, k, d) for kind in ("dir", "sum") for d in range(2)])
            first = own[0, zz] + sum_rx[run, 0, zz].astype(F32) + dir_rx[run, 1, zz].astype(F32)
            second = own[1, zz] + sum_rx[run, 1, zz].astype(F32) + dir_rx[run, 0, zz].astype(F32)
            return first, second

        def z_send(kind, d, value):
            z_tx[run, kind, d] = value.astype(BF16)
            send(("z", run, kind, d), z_tx.at[run, kind, d], z_rx.at[run, kind, d], z_to[d])

        first, second = collect(0)
        z_send(0, 0, first)
        z_send(0, 1, second)
        first, second = collect(1)
        z_send(1, 0, second)
        rows_f32[0] = first
        first, second = collect(2)
        z_send(1, 1, first)
        rows_f32[1] = second
        for d in range(2):
            arrived(("z", run, 0, d))
            z_send(2, d, rows_f32[d] + z_rx[run, 0, d].astype(F32))
        first, second = collect(3)
        arrived(*[("z", run, kind, d) for kind in (1, 2) for d in range(2)])
        first = first + z_rx[run, 2, 0].astype(F32) + z_rx[run, 1, 1].astype(F32)
        second = second + z_rx[run, 2, 1].astype(F32) + z_rx[run, 1, 0].astype(F32)
        return [first, second]

    loads[3].wait()
    loads[4].wait()
    arrived(("halo", 0), ("halo", 1))
    sums = summed_terms(0, wide_v, lambda step: stat_sum(0, step))
    stat_sum(0, 4)
    norm = total_of(0, 0) / cells
    shift = total_of(0, 1) / cells / (norm + EPSILON)

    crossed, squares = [], []
    for j in range(2):
        v = v_rows[j]
        sigma = jnp.where(masks[j], energies[j] * v + scale * sums[j], 0.0)
        u = sigma - shift * v
        wide_u[1 + j, z, y] = u.astype(BF16)
        sigma_out[j] = sigma
        next_out[j] = u
        crossed.append(u * v)
        squares.append(u * u)

    def rows_send(key, j, zz, yy, to):
        part = wide_u.at[1 + j, zz, yy]
        send(key, part, part, to)

    strips = [z, zm, zp, zo]
    across = [y, ym, yp, yo]

    def z_own():
        for first in (True, False):
            for d in range(2):
                j = d if first else 1 - d
                rows_send(("gz", d, j), j, z, y, z_to[d])

    def z_forward(d):
        arrived(("gz", d, d))
        rows_send(("gzf", d), d, zm if d == 0 else zp, y, z_to[d])

    def y_own(k):
        for first in (True, False):
            for d in range(2):
                j = d if first else 1 - d
                rows_send(("gy", k, d, j), j, strips[k], y, y_to[d])

    def y_forward(k):
        for d in range(2):
            arrived(("gy", k, d, d))
            rows_send(("gyf", k, d), d, strips[k], ym if d == 0 else yp, y_to[d])

    def y_rest(k):
        for d in range(2):
            arrived(("gy", k, d, 1 - d))

    def halo(k, m):
        for j in range(2):
            send(
                ("gh", k, m, j),
                wide_u.at[1 + j, strips[k], across[m]],
                wide_u.at[3 if j == 0 else 0, strips[k], across[m]],
                below if j == 0 else above,
            )

    z_own()
    y_own(0)
    halo(0, 0)
    stat_tx[1, 0, 0] = fold(jnp.stack(crossed))
    stat_tx[1, 0, 1] = fold(jnp.stack(squares))
    stat_send(1, 0)
    y_forward(0)
    y_rest(0)
    halo(0, 1)
    halo(0, 2)
    for d in range(2):
        z_forward(d)
    for d in range(2):
        arrived(("gz", d, 1 - d))
    y_own(1)
    y_own(2)
    halo(1, 0)
    halo(2, 0)
    for d in range(2):
        arrived(("gyf", 0, d))
    halo(0, 3)
    stat_sum(1, 0)
    for d in range(2):
        arrived(("gzf", d))
    y_own(3)
    halo(3, 0)
    for k in (1, 2):
        y_forward(k)
        y_rest(k)
        halo(k, 1)
        halo(k, 2)
    y_forward(3)
    y_rest(3)
    halo(3, 1)
    halo(3, 2)
    for k in (1, 2, 3):
        for d in range(2):
            arrived(("gyf", k, d))
        halo(k, 3)
    arrived(*[("gh", k, m, j) for k in range(4) for m in range(4) for j in range(2)])

    sums = summed_terms(1, wide_u, lambda step: stat_sum(1, step + 1))

    cross, square = total_of(1, 0) / cells, total_of(1, 1) / cells
    gap = (cross - shift * EPSILON) / (norm + EPSILON)
    residual_sq = square - 2.0 * gap * cross + gap * gap * norm
    inverse = 1.0 / jnp.sqrt(jnp.maximum(residual_sq, 0.0) + EPSILON)
    for j in range(2):
        u, sigma = next_out[j], sigma_out[j]
        next_out[j] = inverse * (u - gap * v_rows[j])
        applied = jnp.where(masks[j], energies[j] * u + scale * sums[j], 0.0)
        sigma_out[j] = inverse * (applied - gap * sigma)

    for copy in copies.values():
        copy.wait_send()


def on_device(
    dims, lanczos_vector, left_block, right_block, left_energy, right_energy, sector_shifts, sector_sizes
):
    n_z, n_y = dims[3:]
    sectors, block, width = lanczos_vector.shape
    terms = left_block.shape[1]
    span = block // (n_z * n_y)
    strips = (n_z, n_y, span)
    out = jax.ShapeDtypeStruct((sectors, span, width), F32)
    exchange = pltpu.VMEM((2, 2, n_z, span, width), BF16)
    vmem, smem = (pl.BlockSpec(memory_space=s) for s in (pltpu.VMEM, pltpu.SMEM))
    hbm = pl.BlockSpec(memory_space=pl.ANY)
    return pl.pallas_call(
        functools.partial(kernel, dims),
        out_shape=(out, out),
        in_specs=[smem, smem, vmem, vmem, hbm, hbm, hbm],
        out_specs=(vmem, vmem),
        scratch_shapes=[
            pltpu.VMEM((sectors, n_z * n_y, span, width), F32),
            pltpu.VMEM((sectors, span, width), F32),
            pltpu.VMEM((sectors, terms, *strips, width), BF16),
            pltpu.VMEM((sectors, terms, block, width), BF16),
            pltpu.VMEM((5, *strips, width), BF16),
            pltpu.VMEM((5, *strips, width), BF16),
            *[exchange] * 6,
            pltpu.VMEM((2, n_z, span, width), F32),
            pltpu.VMEM((2, n_z, span, width), F32),
            pltpu.VMEM((2, 3, 2, span, width), BF16),
            pltpu.VMEM((2, 3, 2, span, width), BF16),
            pltpu.VMEM((2, span, width), F32),
            pltpu.VMEM((2, 6, 2, 8, 128), F32),
            pltpu.VMEM((2, 5, 3, 2, 8, 128), F32),
            pltpu.SemaphoreType.DMA((5,)),
            pltpu.SemaphoreType.DMA((COPIES,)),
            pltpu.SemaphoreType.DMA((COPIES,)),
        ],
        compiler_params=pltpu.CompilerParams(collective_id=0, has_side_effects=True),
        name="davidson_step",
    )(
        sector_shifts,
        sector_sizes,
        left_energy,
        right_energy,
        lanczos_vector.reshape(sectors, n_z * n_y, span, width),
        left_block.reshape(sectors, terms, *strips, width),
        right_block,
    )


def solution(mesh):
    dims = (2, 4, 2, 4, 4)
    finer = Mesh(mesh.devices.reshape(*dims), (*SECTOR, *TERM))
    return jax.shard_map(
        functools.partial(on_device, dims),
        mesh=finer,
        in_specs=(
            P(SECTOR, None, None),
            P(SECTOR, TERM, None, None),
            P(SECTOR, TERM, None, None),
            P(SECTOR, None),
            P(SECTOR, None),
            P(TERM),
            P(SECTOR),
        ),
        out_specs=(P(SECTOR, TERM, None), P(SECTOR, TERM, None)),
        check_vma=False,
    )
```

time: 284 us -> 89.5 us (0.32)
  the two profiles are of different devices: /device:TPU:3 before, /device:TPU:1 now
where the time goes in v1:
time: 89.5 us; the launch traced here: 89.4 us
  Pallas kernels  85.6 us (96%)
  local copies, waits for them, and re-layouts  3.14 us (4%)
    pallas_call x1, Pallas kernels, on_device(): pl.pallas_call(functools.partial(kernel, dims), out_shape=(out, out), in_...  85.6 us
    unnamed x2, local copies, waits for them, and re-layouts  3.14 us

profile of v1, /device:TPU:1, one launch (start us, length us, event | category | flops | bytes accessed | tf_op | source)
XLA Modules:
  0.0 89.4 jit_solution(3463315526276551040)
XLA Ops:
  0.6 85.6 %davidson_step.1 = (f32[2,32,512]{2,1,0:T(8,128)}, f32[2,32,512]{2,1,0:T(8,128)}) custom-call(s32[4]{0:T(128)} %shifts.1, s32[2]{0:T(128)} %sizes.1, f32[2,512]{1,0:T(2,128)} %left_energy.1, f32[2,512]{1,0:T(2,128)} %right_energy.1, f32[2,16,32,512]{3,2,1,0:T(8,128)} %bitcast.3, bf16[2,4,4,4,32,512]{5,4,3,2,1,0:T(8,128)(2,1)} %bitcast.2, ...), custom_call_target="tpu_custom_call" | custom-call | tf_op jit(solution)/shard_map/davidson_step/pallas_call | solution.py:394
  86.2 1.6 %copy.11 = f32[2,32,512]{2,1,0:T(8,128)} copy(f32[2,32,512]{2,1,0:T(8,128)} %get-tuple-element.4) | data formatting | bytes 262144
  87.8 1.6 %copy.12 = f32[2,32,512]{2,1,0:T(8,128)} copy(f32[2,32,512]{2,1,0:T(8,128)} %get-tuple-element.5) | data formatting | bytes 262144

commit v2 on v1

v2 whole, which is shorter than its diff:
```python
import functools

import jax
import jax.numpy as jnp
from jax import lax
from jax.experimental import pallas as pl
from jax.experimental.pallas import tpu as pltpu
from jax.sharding import Mesh
from jax.sharding import PartitionSpec as P

TERM = ("term_0", "term_1")
SECTOR = ("sector_0", "sector_1", "sector_2")
MESH = pl.DeviceIdType.MESH
F32, BF16 = jnp.float32, jnp.bfloat16
EPSILON = 1e-06
GROUPS, SOURCES = 66, 12


def fold(values):
    total = None
    for j in range(values.shape[0]):
        for r in range(0, values.shape[1], 8):
            for c in range(0, values.shape[2], 128):
                piece = values[j, r : r + 8, c : c + 128]
                total = piece if total is None else total + piece
    return total


def kernel(
    dims,
    shifts_hbm,
    sizes_hbm,
    left_energy_hbm,
    right_energy_hbm,
    v_hbm,
    left_hbm,
    right_hbm,
    next_out,
    sigma_out,
    shifts,
    sizes,
    left_energy,
    right_energy,
    v_full,
    v_rows,
    left,
    right,
    wide_v,
    wide_u,
    opp_tx,
    relay_rx,
    y_tx,
    y_rx,
    near,
    own,
    z_tx,
    z_rx,
    rows_f32,
    mixed,
    turned,
    stat_tx,
    stat_rx,
    load_sem,
    send_sem,
    recv_sem,
):
    n_lo, n_x, n_core, n_z, n_y = dims
    terms = left.shape[1]
    span, width = v_rows.shape[1], v_rows.shape[2]
    n_sec = n_lo * n_x * n_core
    block = n_z * n_y * span
    scale = float(terms * n_z * n_y) ** (-0.5)
    cells = float(2 * n_sec * block * width)

    lo, x, core = [lax.axis_index(a) for a in SECTOR]
    z, y = [lax.axis_index(a) for a in TERM]
    sec = (lo * n_x + x) * n_core + core
    rank = z * n_y + y
    zs = [lax.rem(z + k, n_z) for k in range(n_z)]
    ys = [lax.rem(y + k, n_y) for k in range(n_y)]
    zp, zo, zm = zs[1], zs[2], zs[3]
    yp, yo, ym = ys[1], ys[2], ys[3]
    y_next = [yp, ym]
    y_to = [{"term_1": yp}, {"term_1": ym}]
    z_to = [{"term_0": zp}, {"term_0": zm}]

    def sector_device(s):
        s = lax.rem(s, n_sec)
        return {
            "sector_0": s // (n_x * n_core),
            "sector_1": lax.rem(s // n_core, n_x),
            "sector_2": lax.rem(s, n_core),
        }

    beside = [sector_device(sec + n_sec - 1), sector_device(sec + 1)]


    def pair(i):
        return i + 1 - 2 * lax.rem(i, 2)

    stages = [
        {"sector_2": 1 - core},
        {"sector_1": pair(x)},
        {"sector_1": n_x - 1 - x},
        {"sector_0": 1 - lo},
        {"term_0": pair(z)},
        {"term_0": n_z - 1 - z},
        {"term_1": pair(y)},
        {"term_1": n_y - 1 - y},
    ]
    last_stage = [4, 8]

    barrier = pltpu.get_barrier_semaphore()
    peers = [*beside, *y_to, {"term_1": yo}, *z_to, *stages[1:4]]
    for peer in peers:
        pl.semaphore_signal(barrier, inc=1, device_id=peer, device_id_type=MESH)

    loads = [pltpu.make_async_copy(v_hbm.at[:, rank], v_rows, load_sem.at[0])]
    for j in range(2):
        loads.append(pltpu.make_async_copy(v_hbm.at[j], v_full.at[j], load_sem.at[1 + j]))
    small = [
        (sizes_hbm, sizes),
        (shifts_hbm, shifts),
        (left_energy_hbm, left_energy),
        (right_energy_hbm, right_energy),
    ]
    small = [pltpu.make_async_copy(a, b, load_sem.at[5 + i]) for i, (a, b) in enumerate(small)]
    for load in small:
        load.start()
    loads.append(pltpu.make_async_copy(left_hbm, left, load_sem.at[3]))
    loads.append(pltpu.make_async_copy(right_hbm, right, load_sem.at[4]))
    for load in loads:
        load.start()

    groups, sources = {}, {}

    def send(group, source, src, dst, to):
        pltpu.make_async_remote_copy(
            src_ref=src,
            dst_ref=dst,
            send_sem=send_sem.at[sources.setdefault(source, len(sources))],
            recv_sem=recv_sem.at[groups.setdefault(group, len(groups))],
            device_id=to,
            device_id_type=MESH,
        ).start()

    def arrived(group, like):
        pltpu.make_async_copy(like, like, recv_sem.at[groups[group]]).wait()

    def sent(source, like):
        pltpu.make_async_copy(like, like, send_sem.at[sources[source]]).wait()

    def stat_send(run, stage):
        send(
            ("stat", run, stage),
            ("stat", run),
            stat_tx.at[run, stage],
            stat_rx.at[run, stage],
            stages[stage],
        )

    def stat_sum(run, stage):
        arrived(("stat", run, stage), stat_rx.at[run, stage])
        stat_tx[run, stage + 1] = stat_tx[run, stage] + stat_rx[run, stage]
        if stage + 1 < last_stage[run]:
            stat_send(run, stage + 1)

    def total_of(run, which):
        return jnp.sum(stat_tx[run, last_stage[run], which], keepdims=True)

    for load in small:
        load.wait()
    row = lax.broadcasted_iota(jnp.int32, (span, width), 0) + rank * span
    col = lax.broadcasted_iota(jnp.int32, (span, width), 1)
    masks, energies = [], []
    for j in range(2):
        masks.append((row < sizes[j]) & (col < sizes[j]))
        le = jnp.where(row == col, left_energy[j : j + 1, :], 0.0)
        energies.append(jnp.sum(le, axis=1, keepdims=True) + right_energy[j : j + 1, :])

    zero = jnp.zeros((n_y, span, width), BF16)
    for k in range(n_z):
        wide_v[4, k] = zero
        wide_u[4, k] = zero
    pl.semaphore_wait(barrier, len(peers))
    for j in range(2):
        loads[1 + j].wait()
        for k in range(n_z * n_y):
            r = lax.broadcasted_iota(jnp.int32, (span, width), 0) + k * span
            keep = (r < sizes[j]) & (col < sizes[j])
            wide_v[2 + j, k // n_y, k % n_y] = jnp.where(keep, v_full[j, k], 0.0).astype(BF16)
        send("halo", "halo", wide_v.at[2 + j], wide_v.at[1 - j], beside[j])

    eye = (
        lax.broadcasted_iota(jnp.int32, (span, 128), 0)
        - lax.broadcasted_iota(jnp.int32, (span, 128), 1)
    )
    squares = jnp.zeros((8, 128), F32)
    weighted = jnp.zeros((8, 128), F32)
    for j in range(2):
        for k in range(n_z * n_y):
            at = k * span // 128 * 128
            le = jnp.where(eye == at - k * span, left_energy[j : j + 1, at : at + 128], 0.0)
            energy = jnp.sum(le, axis=1, keepdims=True) + right_energy[j : j + 1, :]
            r = lax.broadcasted_iota(jnp.int32, (span, width), 0) + k * span
            keep = (r < sizes[j]) & (col < sizes[j])
            v = jnp.where(keep, v_full[j, k], 0.0)
            squares = squares + fold((v * v)[None])
            weighted = weighted + fold((v * v * energy)[None])
    stat_tx[0, 0, 0] = squares
    stat_tx[0, 0, 1] = weighted
    stat_send(0, 0)
    loads[0].wait()
    for j in range(2):
        v_rows[j] = jnp.where(masks[j], v_rows[j], 0.0)

    loads[4].wait()
    half = 256
    ones = lax.broadcasted_iota(jnp.int32, (half, half), 0) == lax.broadcasted_iota(
        jnp.int32, (half, half), 1
    )
    ones = ones.astype(F32).astype(BF16)
    for j in range(2):
        for t in range(terms):
            for a in range(0, block, half):
                for b in range(0, width, half):
                    turned[j, t * width + b : t * width + b + half, a : a + half] = lax.dot_general(
                        ones,
                        right[j, t, a : a + half, b : b + half],
                        (((1,), (1,)), ((), ())),
                        preferred_element_type=F32,
                    ).astype(BF16)

    slots = []
    for j in range(2):
        for t in range(terms):
            p = 1 + j + shifts[t]
            outside = ((sec == 0) & (p == 0)) | ((sec == n_sec - 1) & (p == 3))
            slots.append(jnp.where(outside, 4, jnp.where(p == 0, 0, jnp.where(p == 3, 1, p + 1))))

    def chunk(vector, j, yy):
        for t in range(terms):
            rows = left[j, t, :, yy].reshape(n_z * span, block)
            paired = vector[slots[j * terms + t]].reshape(block, width)
            mixed[j, :, t * width : (t + 1) * width] = jnp.dot(
                rows, paired, preferred_element_type=F32
            ).astype(BF16)
        total = jnp.dot(mixed[j], turned[j], preferred_element_type=F32)
        return total.reshape(n_z, span, block)

    def summed_terms(run, vector, between):
        order = [zo, zp, zm, z]
        for d in range(2):
            opp_tx[run, d] = chunk(vector, d, yo).astype(BF16)
            for k, zz in enumerate(order):
                send(
                    ("relay", run, k),
                    ("relay", run),
                    opp_tx.at[run, d, zz],
                    relay_rx.at[run, d, zz],
                    y_to[d] if k else {"term_1": yo},
                )

        def y_send(k, kind, d):
            part = 2 * kind + d
            send(
                ("y", run, k),
                ("y", run),
                y_tx.at[run, part, order[k]],
                y_rx.at[run, part, order[k]],
                y_to[d],
            )

        def relay(k):
            zz = order[k]
            arrived(("relay", run, k), relay_rx.at[run, :, zz])
            for d in range(2):
                y_tx[run, 2 + d, zz] = (near[d, zz] + relay_rx[run, d, zz].astype(F32)).astype(BF16)
                y_send(k, 1, d)

        for d in range(2):
            y_tx[run, d] = chunk(vector, 1 - d, y_next[d]).astype(BF16)
            y_send(0, 0, d)
        for d in range(2):
            near[d] = chunk(vector, d, y_next[d])
            y_tx[run, 2 + d, zo] = near[d, zo].astype(BF16)
            y_send(0, 1, d)
        between(0)
        for k in range(1, n_z):
            for d in range(2):
                y_send(k, 0, d)
            if k < 3:
                own[k - 1] = chunk(vector, k - 1, y)
            relay(k)

        def collect(k):
            zz = order[k]
            arrived(("y", run, k), y_rx.at[run, :, zz])
            first = own[0, zz] + y_rx[run, 2, zz].astype(F32) + y_rx[run, 1, zz].astype(F32)
            second = own[1, zz] + y_rx[run, 3, zz].astype(F32) + y_rx[run, 0, zz].astype(F32)
            if k == 0:
                arrived(("relay", run, 0), relay_rx.at[run, :, zo])
                first = first + relay_rx[run, 0, zo].astype(F32)
                second = second + relay_rx[run, 1, zo].astype(F32)
            return first, second

        def z_send(kind, d, value):
            z_tx[run, kind, d] = value.astype(BF16)
            send(
                ("z", run, min(kind, 1), d if kind == 0 else 0),
                ("z", run),
                z_tx.at[run, kind, d],
                z_rx.at[run, kind, d],
                z_to[d],
            )

        first, second = collect(0)
        z_send(0, 0, first)
        z_send(0, 1, second)
        between(1)
        first, second = collect(1)
        z_send(1, 0, second)
        rows_f32[0] = first
        first, second = collect(2)
        z_send(1, 1, first)
        rows_f32[1] = second
        for d in range(2):
            arrived(("z", run, 0, d), z_rx.at[run, 0, d])
            z_send(2, d, rows_f32[d] + z_rx[run, 0, d].astype(F32))
        between(2)
        first, second = collect(3)
        arrived(("z", run, 1, 0), z_rx.at[run, 1:3])
        between(3)
        first = first + z_rx[run, 2, 0].astype(F32) + z_rx[run, 1, 1].astype(F32)
        second = second + z_rx[run, 2, 1].astype(F32) + z_rx[run, 1, 0].astype(F32)
        return [first, second]

    loads[3].wait()
    arrived("halo", wide_v.at[0:2])
    sums = summed_terms(0, wide_v, lambda step: stat_sum(0, step))
    norm = total_of(0, 0) / cells
    shift = total_of(0, 1) / cells / (norm + EPSILON)

    crossed, squares = [], []
    for j in range(2):
        v = v_rows[j]
        sigma = jnp.where(masks[j], energies[j] * v + scale * sums[j], 0.0)
        u = sigma - shift * v
        wide_u[2 + j, z, y] = u.astype(BF16)
        sigma_out[j] = sigma
        next_out[j] = u
        crossed.append(u * v)
        squares.append(u * u)

    def rows_send(group, source, j, zz, yy, to):
        part = wide_u.at[2 + j, zz, yy]
        send(group, source, part, part, to)

    strips = [z, zm, zp, zo]
    across = [y, ym, yp, yo]

    def rows_arrived(group, j, zz, yy):
        arrived(group, wide_u.at[2 + j, zz, yy])

    def z_forward(d):
        zz = (zm, zp)[d]
        rows_arrived(("gz", d, d), d, zz, y)
        rows_send(("gzf", d), "gz", d, zz, y, z_to[d])

    def y_own(k):
        for first in (True, False):
            for d in range(2):
                j = d if first else 1 - d
                rows_send(("gy", k, d, j), "gy", j, strips[k], y, y_to[d])

    def y_forward(k):
        for d in range(2):
            rows_arrived(("gy", k, d, d), d, strips[k], (ym, yp)[d])
            rows_send(("gyf", k, d), "gy", d, strips[k], (ym, yp)[d], y_to[d])

    def y_rest(k):
        for d in range(2):
            rows_arrived(("gy", k, d, 1 - d), 1 - d, strips[k], (ym, yp)[d])

    def y_last(k):
        for d in range(2):
            rows_arrived(("gyf", k, d), d, strips[k], yo)

    def halo(k, m):
        for j in range(2):
            part = (strips[k], across[m])
            send("gh", "gh", wide_u.at[2 + j, *part], wide_u.at[1 - j, *part], beside[j])

    for first in (True, False):
        for d in range(2):
            j = d if first else 1 - d
            rows_send(("gz", d, j), "gz", j, z, y, z_to[d])
    y_own(0)
    halo(0, 0)
    stat_tx[1, 0, 0] = fold(jnp.stack(crossed))
    stat_tx[1, 0, 1] = fold(jnp.stack(squares))
    stat_send(1, 0)
    y_forward(0)
    y_rest(0)
    halo(0, 1)
    halo(0, 2)
    for d in range(2):
        z_forward(d)
    for d in range(2):
        rows_arrived(("gz", d, 1 - d), 1 - d, (zm, zp)[d], y)
    y_own(1)
    y_own(2)
    halo(1, 0)
    halo(2, 0)
    stat_sum(1, 0)
    y_last(0)
    halo(0, 3)
    for d in range(2):
        rows_arrived(("gzf", d), d, zo, y)
    for j in range(2):
        rows_send(("gyf", 3, j), "gy", j, zo, y, {"term_1": yo})
    y_own(3)
    halo(3, 0)
    stat_sum(1, 1)
    for k in (1, 2):
        y_forward(k)
        y_rest(k)
        halo(k, 1)
        halo(k, 2)
    for d in range(2):
        rows_arrived(("gy", 3, d, d), d, zo, (ym, yp)[d])
    y_rest(3)
    halo(3, 1)
    halo(3, 2)
    stat_sum(1, 2)
    for k in (1, 2, 3):
        y_last(k)
        halo(k, 3)
    stat_sum(1, 3)
    arrived("gh", wide_u.at[0:2])

    sums = summed_terms(1, wide_u, lambda step: stat_sum(1, step + 4))

    cross, square = total_of(1, 0) / cells, total_of(1, 1) / cells
    gap = (cross - shift * EPSILON) / (norm + EPSILON)
    residual_sq = square - 2.0 * gap * cross + gap * gap * norm
    inverse = 1.0 / jnp.sqrt(jnp.maximum(residual_sq, 0.0) + EPSILON)
    for j in range(2):
        u, sigma = next_out[j], sigma_out[j]
        next_out[j] = inverse * (u - gap * v_rows[j])
        applied = jnp.where(masks[j], energies[j] * u + scale * sums[j], 0.0)
        sigma_out[j] = inverse * (applied - gap * sigma)

    sent("halo", wide_v.at[2:4])
    for run in range(2):
        sent(("relay", run), opp_tx.at[run])
        sent(("y", run), y_tx.at[run])
        sent(("z", run), z_tx.at[run])
        sent(("stat", run), stat_tx.at[run, 0 : last_stage[run]])
    sent("gz", z_tx.at[0])
    sent("gy", left.at[0, 0:2, 0:3])
    sent("gh", wide_u.at[2:4])


def on_device(
    dims, lanczos_vector, left_block, right_block, left_energy, right_energy, sector_shifts, sector_sizes
):
    n_z, n_y = dims[3:]
    sectors, block, width = lanczos_vector.shape
    terms = left_block.shape[1]
    span = block // (n_z * n_y)
    strips = (n_z, n_y, span)
    out = pltpu.VMEM((sectors, span, width), F32)
    exchange = [pltpu.VMEM((2, parts, n_z, span, width), BF16) for parts in (2, 2, 4, 4)]
    vmem = pl.BlockSpec(memory_space=pltpu.VMEM)
    hbm = pl.BlockSpec(memory_space=pl.ANY)
    return pl.pallas_call(
        functools.partial(kernel, dims),
        out_shape=(out, out),
        in_specs=[hbm] * 7,
        out_specs=(vmem, vmem),
        scratch_shapes=[
            pltpu.SMEM((terms,), jnp.int32),
            pltpu.SMEM((sectors,), jnp.int32),
            pltpu.VMEM((sectors, block), F32),
            pltpu.VMEM((sectors, width), F32),
            pltpu.VMEM((sectors, n_z * n_y, span, width), F32),
            pltpu.VMEM((sectors, span, width), F32),
            pltpu.VMEM((sectors, terms, *strips, width), BF16),
            pltpu.VMEM((sectors, terms, block, width), BF16),
            pltpu.VMEM((5, *strips, width), BF16),
            pltpu.VMEM((5, *strips, width), BF16),
            *exchange,
            pltpu.VMEM((2, n_z, span, width), F32),
            pltpu.VMEM((2, n_z, span, width), F32),
            pltpu.VMEM((2, 3, 2, span, width), BF16),
            pltpu.VMEM((2, 3, 2, span, width), BF16),
            pltpu.VMEM((2, span, width), F32),
            pltpu.VMEM((sectors, n_z * span, terms * width), BF16),
            pltpu.VMEM((sectors, terms * width, block), BF16),
            pltpu.VMEM((2, 9, 2, 8, 128), F32),
            pltpu.VMEM((2, 8, 2, 8, 128), F32),
            pltpu.SemaphoreType.DMA((9,)),
            pltpu.SemaphoreType.DMA((SOURCES,)),
            pltpu.SemaphoreType.DMA((GROUPS,)),
        ],
        compiler_params=pltpu.CompilerParams(collective_id=0, has_side_effects=True),
        name="davidson_step",
    )(
        sector_shifts,
        sector_sizes,
        left_energy,
        right_energy,
        lanczos_vector.reshape(sectors, n_z * n_y, span, width),
        left_block.reshape(sectors, terms, *strips, width),
        right_block,
    )


def solution(mesh):
    dims = (2, 4, 2, 4, 4)
    finer = Mesh(mesh.devices.reshape(*dims), (*SECTOR, *TERM))
    return jax.shard_map(
        functools.partial(on_device, dims),
        mesh=finer,
        in_specs=(
            P(SECTOR, None, None),
            P(SECTOR, TERM, None, None),
            P(SECTOR, TERM, None, None),
            P(SECTOR, None),
            P(SECTOR, None),
            P(TERM),
            P(SECTOR),
        ),
        out_specs=(P(SECTOR, TERM, None), P(SECTOR, TERM, None)),
        check_vma=False,
    )
```

time: 89.5 us -> 69.4 us (0.78)
  Pallas kernels: 85.6 us -> 66.6 us
  local copies, waits for them, and re-layouts: 3.14 us -> 1.31 us
    pallas_call x1, Pallas kernels: 85.6 us -> 66.6 us  [on_device(): pl.pallas_call(functools.partial(kernel, dims), out_shape=(out, out), in_...]
    unnamed x2, local copies, waits for them, and re-layouts: 3.14 us -> 1.31 us
where the time goes in v2:
time: 69.4 us; the launch traced here: 68.6 us
  Pallas kernels  66.6 us (96%)
  local copies, waits for them, and re-layouts  1.31 us (2%)
    pallas_call x1, Pallas kernels, on_device(): pl.pallas_call(functools.partial(kernel, dims), out_shape=(out, out), in_...  66.6 us

profile of v2, /device:TPU:1, one launch (start us, length us, event | category | flops | bytes accessed | tf_op | source)
XLA Modules:
  0.0 68.6 jit_solution(5922170419284402915)
XLA Ops:
  0.6 66.6 %davidson_step.1 = (f32[2,32,512]{2,1,0:T(8,128)S(1)}, f32[2,32,512]{2,1,0:T(8,128)S(1)}) custom-call(s32[4]{0:T(128)} %shifts_hbm.1, s32[2]{0:T(128)} %sizes_hbm.1, f32[2,512]{1,0:T(2,128)} %left_energy_hbm.1, f32[2,512]{1,0:T(2,128)} %right_energy_hbm.1, f32[2,16,32,512]{3,2,1,0:T(8,128)} %bitcast.3, bf16[2,4,4,4,32,512]{5,4,3,2,1,0:T(8,128)(2,1)} %bitcast.2, ...), custom_call_target="tpu_custom_call" | custom-call | tf_op jit(solution)/shard_map/davidson_step/pallas_call | solution.py:477
  67.2 0.7 copy.11
  67.9 0.7 copy.12

commit v3 on v2

--- a/solution.py
+++ b/solution.py
@@ -13,7 +13,7 @@
 MESH = pl.DeviceIdType.MESH
 F32, BF16 = jnp.float32, jnp.bfloat16
 EPSILON = 1e-06
-GROUPS, SOURCES = 66, 12
+GROUPS, SOURCES = 66, 13
 
 
 def fold(values):
@@ -93,15 +93,17 @@
         }
 
     beside = [sector_device(sec + n_sec - 1), sector_device(sec + 1)]
+    outer = sector_device(sec + n_sec - 1 + 2 * core)
+    outer = [{**outer, "term_1": yy} for yy in ys[1:]]
 
 
     def pair(i):
         return i + 1 - 2 * lax.rem(i, 2)
 
     stages = [
-        {"sector_2": 1 - core},
         {"sector_1": pair(x)},
         {"sector_1": n_x - 1 - x},
+        {"sector_2": 1 - core},
         {"sector_0": 1 - lo},
         {"term_0": pair(z)},
         {"term_0": n_z - 1 - z},
@@ -111,7 +113,7 @@
     last_stage = [4, 8]
 
     barrier = pltpu.get_barrier_semaphore()
-    peers = [*beside, *y_to, {"term_1": yo}, *z_to, *stages[1:4]]
+    peers = [*beside, *y_to, {"term_1": yo}, *z_to, *outer, *stages[:2], stages[3]]
     for peer in peers:
         pl.semaphore_signal(barrier, inc=1, device_id=peer, device_id_type=MESH)
 
@@ -367,16 +369,18 @@
         rows_arrived(("gz", d, d), d, zz, y)
         rows_send(("gzf", d), "gz", d, zz, y, z_to[d])
 
-    def y_own(k):
-        for first in (True, False):
-            for d in range(2):
-                j = d if first else 1 - d
-                rows_send(("gy", k, d, j), "gy", j, strips[k], y, y_to[d])
+    def y_far(k):
+        for j in range(2):
+            rows_send(("gyf", k, j), "gyf", j, strips[k], y, {"term_1": yo})
+
+    def y_near(k, j):
+        for d in (j, 1 - j):
+            rows_send(("gy", k, d, j), "gy", j, strips[k], y, y_to[d])
 
     def y_forward(k):
         for d in range(2):
             rows_arrived(("gy", k, d, d), d, strips[k], (ym, yp)[d])
-            rows_send(("gyf", k, d), "gy", d, strips[k], (ym, yp)[d], y_to[d])
+            rows_send(("gyf", k, d), "gyf", d, strips[k], (ym, yp)[d], y_to[d])
 
     def y_rest(k):
         for d in range(2):
@@ -386,57 +390,79 @@
         for d in range(2):
             rows_arrived(("gyf", k, d), d, strips[k], yo)
 
+    def halo_send(j, k, m, to):
+        part = (strips[k], across[m])
+        send("gh", "gh", wide_u.at[2 + j, *part], wide_u.at[1 - j, *part], to)
+
     def halo(k, m):
-        for j in range(2):
-            part = (strips[k], across[m])
-            send("gh", "gh", wide_u.at[2 + j, *part], wide_u.at[1 - j, *part], beside[j])
+        halo_send(1, k, m, beside[1])
+        if k < 3 or m == 0:
+            halo_send(0, k, m, beside[0])
+        else:
+
+            @pl.when(core == 1)
+            def _():
+                halo_send(0, k, m, beside[0])
+
+        if k == 3 and m == 0:
+
+            @pl.when(core == 0)
+            def _():
+                for to in outer:
+                    halo_send(0, k, m, to)
 
     for first in (True, False):
         for d in range(2):
             j = d if first else 1 - d
             rows_send(("gz", d, j), "gz", j, z, y, z_to[d])
-    y_own(0)
+    for j in range(2):
+        y_near(0, j)
+    y_far(0)
     halo(0, 0)
     stat_tx[1, 0, 0] = fold(jnp.stack(crossed))
     stat_tx[1, 0, 1] = fold(jnp.stack(squares))
     stat_send(1, 0)
-    y_forward(0)
+    for d in range(2):
+        z_forward(d)
+        y_near(1 + d, d)
+    stat_sum(1, 0)
+    for d in range(2):
+        rows_arrived(("gz", d, 1 - d), 1 - d, (zm, zp)[d], y)
+        y_near(1 + d, 1 - d)
+    halo(1, 0)
+    halo(2, 0)
+    for d in range(2):
+        rows_arrived(("gy", 0, d, d), d, z, (ym, yp)[d])
     y_rest(0)
     halo(0, 1)
     halo(0, 2)
-    for d in range(2):
-        z_forward(d)
-    for d in range(2):
-        rows_arrived(("gz", d, 1 - d), 1 - d, (zm, zp)[d], y)
-    y_own(1)
-    y_own(2)
-    halo(1, 0)
-    halo(2, 0)
-    stat_sum(1, 0)
     y_last(0)
     halo(0, 3)
+    y_forward(1)
+    stat_sum(1, 1)
+    y_forward(2)
     for d in range(2):
         rows_arrived(("gzf", d), d, zo, y)
-    for j in range(2):
-        rows_send(("gyf", 3, j), "gy", j, zo, y, {"term_1": yo})
-    y_own(3)
+    y_far(3)
+    for j in range(2):
+        y_near(3, j)
     halo(3, 0)
-    stat_sum(1, 1)
+    stat_sum(1, 2)
     for k in (1, 2):
-        y_forward(k)
         y_rest(k)
         halo(k, 1)
         halo(k, 2)
+    for k in (1, 2):
+        y_last(k)
+        halo(k, 3)
     for d in range(2):
         rows_arrived(("gy", 3, d, d), d, zo, (ym, yp)[d])
     y_rest(3)
     halo(3, 1)
     halo(3, 2)
-    stat_sum(1, 2)
-    for k in (1, 2, 3):
-        y_last(k)
-        halo(k, 3)
     stat_sum(1, 3)
+    y_last(3)
+    halo(3, 3)
     arrived("gh", wide_u.at[0:2])
 
     sums = summed_terms(1, wide_u, lambda step: stat_sum(1, step + 4))
@@ -458,7 +484,8 @@
         sent(("z", run), z_tx.at[run])
         sent(("stat", run), stat_tx.at[run, 0 : last_stage[run]])
     sent("gz", z_tx.at[0])
-    sent("gy", left.at[0, 0:2, 0:3])
+    sent("gy", y_tx.at[0])
+    sent("gyf", opp_tx.at[0])
     sent("gh", wide_u.at[2:4])
 
 

time: 69.4 us -> 70.9 us (1.022)
  Pallas kernels: 66.6 us -> 68.7 us
    pallas_call x1, Pallas kernels: 66.6 us -> 68.7 us  [on_device(): pl.pallas_call(functools.partial(kernel, dims), out_shape=(out, out), in_...]
where the time goes in v3:
time: 70.9 us; the launch traced here: 70.7 us
  Pallas kernels  68.7 us (97%)
  local copies, waits for them, and re-layouts  1.31 us (2%)
    pallas_call x1, Pallas kernels, on_device(): pl.pallas_call(functools.partial(kernel, dims), out_shape=(out, out), in_...  68.7 us

profile of v3, /device:TPU:1, one launch (start us, length us, event | category | flops | bytes accessed | tf_op | source)
XLA Modules:
  0.0 70.7 jit_solution(9736055181156611549)
XLA Ops:
  0.6 68.7 %davidson_step.1 = (f32[2,32,512]{2,1,0:T(8,128)S(1)}, f32[2,32,512]{2,1,0:T(8,128)S(1)}) custom-call(s32[4]{0:T(128)} %shifts_hbm.1, s32[2]{0:T(128)} %sizes_hbm.1, f32[2,512]{1,0:T(2,128)} %left_energy_hbm.1, f32[2,512]{1,0:T(2,128)} %right_energy_hbm.1, f32[2,16,32,512]{3,2,1,0:T(8,128)} %bitcast.3, bf16[2,4,4,4,32,512]{5,4,3,2,1,0:T(8,128)(2,1)} %bitcast.2, ...), custom_call_target="tpu_custom_call" | custom-call | tf_op jit(solution)/shard_map/davidson_step/pallas_call | solution.py:504
  69.4 0.7 copy.11
  70.0 0.7 copy.12

commit v4 on v2

--- a/solution.py
+++ b/solution.py
@@ -93,16 +93,18 @@
         }
 
     beside = [sector_device(sec + n_sec - 1), sector_device(sec + 1)]
+    first_one, last_one = sec == 0, sec == n_sec - 1
+    at_end = first_one | last_one
 
 
     def pair(i):
         return i + 1 - 2 * lax.rem(i, 2)
 
     stages = [
-        {"sector_2": 1 - core},
         {"sector_1": pair(x)},
         {"sector_1": n_x - 1 - x},
         {"sector_0": 1 - lo},
+        {"sector_2": 1 - core},
         {"term_0": pair(z)},
         {"term_0": n_z - 1 - z},
         {"term_1": pair(y)},
@@ -111,7 +113,7 @@
     last_stage = [4, 8]
 
     barrier = pltpu.get_barrier_semaphore()
-    peers = [*beside, *y_to, {"term_1": yo}, *z_to, *stages[1:4]]
+    peers = [*beside, *y_to, {"term_1": yo}, *z_to, *stages[:3]]
     for peer in peers:
         pl.semaphore_signal(barrier, inc=1, device_id=peer, device_id_type=MESH)
 
@@ -147,6 +149,10 @@
     def arrived(group, like):
         pltpu.make_async_copy(like, like, recv_sem.at[groups[group]]).wait()
 
+    def end_or_both(wait, key, like):
+        pl.when(at_end)(lambda: wait(key, like.at[0:1]))
+        pl.when(jnp.logical_not(at_end))(lambda: wait(key, like))
+
     def sent(source, like):
         pltpu.make_async_copy(like, like, send_sem.at[sources[source]]).wait()
 
@@ -182,6 +188,14 @@
     for k in range(n_z):
         wide_v[4, k] = zero
         wide_u[4, k] = zero
+    for slot, here in enumerate((first_one, last_one)):
+
+        @pl.when(here)
+        def _():
+            for k in range(n_z):
+                wide_v[slot, k] = zero
+                wide_u[slot, k] = zero
+
     pl.semaphore_wait(barrier, len(peers))
     for j in range(2):
         loads[1 + j].wait()
@@ -189,7 +203,11 @@
             r = lax.broadcasted_iota(jnp.int32, (span, width), 0) + k * span
             keep = (r < sizes[j]) & (col < sizes[j])
             wide_v[2 + j, k // n_y, k % n_y] = jnp.where(keep, v_full[j, k], 0.0).astype(BF16)
-        send("halo", "halo", wide_v.at[2 + j], wide_v.at[1 - j], beside[j])
+
+        @pl.when(jnp.logical_not((first_one, last_one)[j]))
+        def _():
+            send("halo", "halo", wide_v.at[2 + j], wide_v.at[1 - j], beside[j])
+
 
     eye = (
         lax.broadcasted_iota(jnp.int32, (span, 128), 0)
@@ -336,7 +354,7 @@
         return [first, second]
 
     loads[3].wait()
-    arrived("halo", wide_v.at[0:2])
+    end_or_both(arrived, "halo", wide_v.at[0:2])
     sums = summed_terms(0, wide_v, lambda step: stat_sum(0, step))
     norm = total_of(0, 0) / cells
     shift = total_of(0, 1) / cells / (norm + EPSILON)
@@ -389,7 +407,11 @@
     def halo(k, m):
         for j in range(2):
             part = (strips[k], across[m])
-            send("gh", "gh", wide_u.at[2 + j, *part], wide_u.at[1 - j, *part], beside[j])
+
+            @pl.when(jnp.logical_not((first_one, last_one)[j]))
+            def _():
+                send("gh", "gh", wide_u.at[2 + j, *part], wide_u.at[1 - j, *part], beside[j])
+
 
     for first in (True, False):
         for d in range(2):
@@ -437,7 +459,7 @@
         y_last(k)
         halo(k, 3)
     stat_sum(1, 3)
-    arrived("gh", wide_u.at[0:2])
+    end_or_both(arrived, "gh", wide_u.at[0:2])
 
     sums = summed_terms(1, wide_u, lambda step: stat_sum(1, step + 4))
 
@@ -451,7 +473,7 @@
         applied = jnp.where(masks[j], energies[j] * u + scale * sums[j], 0.0)
         sigma_out[j] = inverse * (applied - gap * sigma)
 
-    sent("halo", wide_v.at[2:4])
+    end_or_both(sent, "halo", wide_v.at[2:4])
     for run in range(2):
         sent(("relay", run), opp_tx.at[run])
         sent(("y", run), y_tx.at[run])
@@ -459,7 +481,16 @@
         sent(("stat", run), stat_tx.at[run, 0 : last_stage[run]])
     sent("gz", z_tx.at[0])
     sent("gy", left.at[0, 0:2, 0:3])
-    sent("gh", wide_u.at[2:4])
+    end_or_both(sent, "gh", wide_u.at[2:4])
+
+
+def write_out(next_in, sigma_in, next_out, sigma_out, sem):
+    pairs = ((next_in, next_out), (sigma_in, sigma_out))
+    copies = [pltpu.make_async_copy(a, b, sem.at[i]) for i, (a, b) in enumerate(pairs)]
+    for copy in copies:
+        copy.start()
+    for copy in copies:
+        copy.wait()
 
 
 def on_device(
@@ -474,7 +505,7 @@
     exchange = [pltpu.VMEM((2, parts, n_z, span, width), BF16) for parts in (2, 2, 4, 4)]
     vmem = pl.BlockSpec(memory_space=pltpu.VMEM)
     hbm = pl.BlockSpec(memory_space=pl.ANY)
-    return pl.pallas_call(
+    results = pl.pallas_call(
         functools.partial(kernel, dims),
         out_shape=(out, out),
         in_specs=[hbm] * 7,
@@ -515,6 +546,16 @@
         left_block.reshape(sectors, terms, *strips, width),
         right_block,
     )
+    whole = jax.ShapeDtypeStruct((sectors, span, width), F32)
+    return pl.pallas_call(
+        write_out,
+        out_shape=(whole, whole),
+        in_specs=[hbm, hbm],
+        out_specs=(hbm, hbm),
+        scratch_shapes=[pltpu.SemaphoreType.DMA((2,))],
+        compiler_params=pltpu.CompilerParams(vmem_limit_bytes=1 << 20),
+        name="write_out",
+    )(*results)
 
 
 def solution(mesh):

time: 69.4 us -> 68.7 us (0.990)
  local copies, waits for them, and re-layouts: 1.31 us -> 0 us
  Pallas kernels: 66.6 us -> 67.6 us
    unnamed x2 -> x0, local copies, waits for them, and re-layouts: 1.31 us -> none
    pallas_call x0 -> x1, Pallas kernels: none -> 0.72 us  [on_device(): pl.pallas_call(write_out, out_shape=(whole, whole), in_specs=[hbm, hbm],...]
where the time goes in v4:
time: 68.7 us; the launch traced here: 68.3 us
  Pallas kernels  67.6 us (98%)
    pallas_call x1, Pallas kernels, on_device(): pl.pallas_call(functools.partial(kernel, dims), out_shape=(out, out), in_...  66.9 us

profile of v4, /device:TPU:1, one launch (start us, length us, event | category | flops | bytes accessed | tf_op | source)
XLA Modules:
  0.0 68.3 jit_solution(10382943217662941411)
XLA Ops:
  0.6 66.9 %davidson_step.1 = (f32[2,32,512]{2,1,0:T(8,128)S(1)}, f32[2,32,512]{2,1,0:T(8,128)S(1)}) custom-call(s32[4]{0:T(128)} %shifts_hbm.1, s32[2]{0:T(128)} %sizes_hbm.1, f32[2,512]{1,0:T(2,128)} %left_energy_hbm.1, f32[2,512]{1,0:T(2,128)} %right_energy_hbm.1, f32[2,16,32,512]{3,2,1,0:T(8,128)} %bitcast.3, bf16[2,4,4,4,32,512]{5,4,3,2,1,0:T(8,128)(2,1)} %bitcast.2, ...), custom_call_target="tpu_custom_call" | custom-call | tf_op jit(solution)/shard_map/davidson_step/pallas_call | solution.py:508
  67.5 0.7 %write_out.1 = (f32[2,32,512]{2,1,0:T(8,128)}, f32[2,32,512]{2,1,0:T(8,128)}) custom-call(f32[2,32,512]{2,1,0:T(8,128)S(1)} %get-tuple-element.4.next_in, f32[2,32,512]{2,1,0:T(8,128)S(1)} %get-tuple-element.5.sigma_in), custom_call_target="tpu_custom_call" | custom-call | tf_op jit(solution)/shard_map/write_out/pallas_call | solution.py:550

commit v5 on v4

--- a/solution.py
+++ b/solution.py
@@ -437,11 +437,11 @@
     stat_sum(1, 0)
     y_last(0)
     halo(0, 3)
-    for d in range(2):
-        rows_arrived(("gzf", d), d, zo, y)
-    for j in range(2):
+    for j in range(2):
+        rows_arrived(("gzf", j), j, zo, y)
         rows_send(("gyf", 3, j), "gy", j, zo, y, {"term_1": yo})
-    y_own(3)
+        for d in (j, 1 - j):
+            rows_send(("gy", 3, d, j), "gy", j, zo, y, y_to[d])
     halo(3, 0)
     stat_sum(1, 1)
     for k in (1, 2):

time: 68.7 us -> 68.1 us (level)
  no operation moved by 1% of the time
where the time goes in v5:
time: 68.1 us; the launch traced here: 68 us
  Pallas kernels  67.4 us (99%)
    pallas_call x1, Pallas kernels, on_device(): pl.pallas_call(functools.partial(kernel, dims), out_shape=(out, out), in_...  66.7 us

profile of v5, /device:TPU:1, one launch (start us, length us, event | category | flops | bytes accessed | tf_op | source)
XLA Modules:
  0.0 68.0 jit_solution(12627228218957949526)
XLA Ops:
  0.6 66.7 %davidson_step.1 = (f32[2,32,512]{2,1,0:T(8,128)S(1)}, f32[2,32,512]{2,1,0:T(8,128)S(1)}) custom-call(s32[4]{0:T(128)} %shifts_hbm.1, s32[2]{0:T(128)} %sizes_hbm.1, f32[2,512]{1,0:T(2,128)} %left_energy_hbm.1, f32[2,512]{1,0:T(2,128)} %right_energy_hbm.1, f32[2,16,32,512]{3,2,1,0:T(8,128)} %bitcast.3, bf16[2,4,4,4,32,512]{5,4,3,2,1,0:T(8,128)(2,1)} %bitcast.2, ...), custom_call_target="tpu_custom_call" | custom-call | tf_op jit(solution)/shard_map/davidson_step/pallas_call | solution.py:508
  67.3 0.7 %write_out.1 = (f32[2,32,512]{2,1,0:T(8,128)}, f32[2,32,512]{2,1,0:T(8,128)}) custom-call(f32[2,32,512]{2,1,0:T(8,128)S(1)} %get-tuple-element.4.next_in, f32[2,32,512]{2,1,0:T(8,128)S(1)} %get-tuple-element.5.sigma_in), custom_call_target="tpu_custom_call" | custom-call | tf_op jit(solution)/shard_map/write_out/pallas_call | solution.py:550
